TPU v7x, 256 devices: a whole 4x4x8 slice. The times are simulated.
256 devices in a mesh: dp: 16 (over y, x), expert: 16 (over z, core).
Axes of the slice: x: 4, y: 4, z: 8, core: 2. Of those that a mesh axis runs over, the one named last changes fastest.
Arguments:
- tokens: bfloat16 [4096, 4096], P('dp', 'expert'), may hold values from -6 to 6
- routing: int32 [4096, 2], P('dp'), may hold values from 0 to 15, all different within a row; in each aligned block of 256 rows (0 to 255, 256 to 511, ...) at most 48 rows name the same one
- gate_weight: bfloat16 [4096, 16], P('expert'), may hold values from -0.09375 to 0.09375
- expert_in: bfloat16 [16, 4096, 8192], P('dp', None, 'expert'), may hold values from -0.09375 to 0.09375
- expert_out: bfloat16 [16, 8192, 4096], P('dp', 'expert'), may hold values from -0.75 to 0.75
Outputs:
- mixed: bfloat16 [4096, 4096], P('dp', 'expert')
Inputs may be any that keep to these rules, and one draw needn't show every extreme that they name: `routing`: each row names two different experts. Within the 256 rows of one group, no expert is named by more than 48 rows, a bound that some block reaches.
All inputs are finite; a program needn't handle non-finite values.
Results may differ from a plain program's by a relative error of at most 0.02.
Values may be sent and summed in bfloat16 or wider, within the bound.
A program may use at most 64 MiB of HBM per device.

v0:
```python
import jax
import jax.numpy as jnp
from jax import lax
from jax.sharding import Mesh
from jax.sharding import PartitionSpec as P

EXPERT = ("expert_0", "expert_1")


def over_axes(value, axes):
    for axis in axes:
        value = lax.psum(value, axis)
    return value


def softmax_rows(logits):
    raised = jnp.exp(logits)
    return raised / jnp.sum(raised, axis=-1, keepdims=True)


def pick_chosen(softmax_all, picks):
    experts = softmax_all.shape[1]
    labels = lax.broadcasted_iota(jnp.int32, (picks.shape[0], 2, experts), 2)
    selected = labels == picks[:, :, None]
    return jnp.sum(jnp.where(selected, softmax_all[:, None, :], 0.0), axis=-1).astype(jnp.bfloat16)


def expert_rows(block_rows, weight_in, weight_out):
    sources = block_rows.shape[0]
    slots_here = block_rows.shape[1]
    width_local = block_rows.shape[2]
    flat_rows = block_rows.reshape(sources * slots_here, width_local)
    pre_act = jnp.dot(
        lax.all_gather(flat_rows, EXPERT, axis=1, tiled=True),
        weight_in,
        preferred_element_type=jnp.float32,
    )
    hidden = jax.nn.gelu(pre_act, approximate=True).astype(jnp.bfloat16)
    partial_out = jnp.dot(hidden, weight_out, preferred_element_type=jnp.float32)
    summed = lax.psum_scatter(
        partial_out.astype(jnp.bfloat16), EXPERT, scatter_dimension=1, tiled=True
    )
    return summed.reshape(sources, slots_here, width_local)


def shards(tokens, routing, gate_weight, expert_in, expert_out):
    group_size = tokens.shape[0]
    width_local = tokens.shape[1]
    experts = gate_weight.shape[1]
    dp_count = lax.axis_size("dp")
    capacity = 3 * group_size // dp_count
    weight_in = expert_in[0]
    weight_out = expert_out[0]
    partial_logits = jnp.dot(tokens, gate_weight, preferred_element_type=jnp.float32)
    logits = over_axes(partial_logits, EXPERT)
    chosen = pick_chosen(softmax_rows(logits), routing)
    order = jnp.concatenate([routing[:, 0], routing[:, 1]], axis=0)
    labels = lax.broadcasted_iota(jnp.int32, (2 * group_size, experts), 1)
    onehot = (labels == order[:, None]).astype(jnp.int32)
    before = jnp.cumsum(onehot, axis=0) - onehot
    slot_flat = jnp.sum(before * onehot, axis=1)
    slot_index = jnp.stack([slot_flat[:group_size], slot_flat[group_size:]], axis=1)
    target = routing * capacity + slot_index
    columns = lax.broadcasted_iota(jnp.int32, (group_size, experts * capacity), 1)
    first_hit = columns == target[:, 0:1]
    second_hit = columns == target[:, 1:2]
    assign = jnp.logical_or(first_hit, second_hit).astype(jnp.bfloat16)
    outgoing = jnp.einsum("gs,gd->sd", assign, tokens, preferred_element_type=jnp.float32)
    outgoing = outgoing.astype(jnp.bfloat16).reshape(experts, capacity, width_local)
    incoming = lax.all_to_all(outgoing, "dp", split_axis=0, concat_axis=0, tiled=True)
    processed = expert_rows(incoming, weight_in, weight_out)
    returned_rows = lax.all_to_all(processed, "dp", split_axis=0, concat_axis=0, tiled=True)
    zero_weight = jnp.zeros((), jnp.bfloat16)
    combine = jnp.where(first_hit, chosen[:, 0:1], zero_weight) + jnp.where(
        second_hit, chosen[:, 1:2], zero_weight
    )
    mixed = jnp.dot(
        combine,
        returned_rows.reshape(experts * capacity, width_local),
        preferred_element_type=jnp.float32,
    )
    return mixed.astype(jnp.bfloat16)


def solution(mesh):
    torus = Mesh(mesh.devices.reshape(mesh.shape["dp"], 8, 2), ("dp", "expert_0", "expert_1"))
    placed = (
        P("dp", EXPERT),
        P("dp", None),
        P(EXPERT, None),
        P("dp", None, EXPERT),
        P("dp", EXPERT, None),
    )
    return jax.shard_map(
        shards, mesh=torus, in_specs=placed, out_specs=P("dp", EXPERT), check_vma=False
    )
```

profile of v0, /device:TPU:2, one launch (start us, length us, event | category | flops | bytes accessed | tf_op | source)
XLA Modules:
  0.0 186.2 jit_solution(17316833488895113456)
XLA Ops:
  6.5 0.0 copy-start
  6.5 0.0 all-gather.2.cloned.1.call-start
  6.5 0.8 fusion.44
  7.3 1.2 reduce-window.6
  8.5 0.2 slice_reduce_fusion
  8.7 0.1 fusion.35
  8.9 0.7 add_add_fusion
  9.6 0.0 copy-done
  9.6 0.6 convolution_convert_fusion.1
  10.2 16.1 %all_to_all.10 = bf16[16,48,256]{2,1,0:T(8,128)(2,1)} all-to-all(bf16[16,48,256]{2,1,0:T(8,128)(2,1)S(1)} %bitcast.49), channel_id=1, replica_groups=mesh['dp'=16,'expert_0'=8,'expert_1'=2] {'dp'}, dimensions={0} | all-to-all | bytes 786432 | tf_op jit(solution)/shard_map/all_to_all | solution.py:70
  26.3 0.0 all-gather.2.cloned.1.call-update
  26.3 0.0 reduce-scatter.2.cloned.1.call-start
  26.3 57.0 %all-gather.2.cloned.1.call-done = bf16[768,4096]{1,0:T(8,128)(2,1)} async-done(((bf16[768,256]{1,0:T(8,128)(2,1)}), bf16[768,4096]{1,0:T(8,128)(2,1)}) %all-gather.2.cloned.1.call-update) | async-done | bytes 6291472 | tf_op jit(solution)/shard_map/all_gather | solution.py:34
  83.3 13.2 %convolution_convert_fusion = bf16[768,4096]{1,0:T(8,128)(2,1)} fusion(bf16[1,512,4096]{2,1,0:T(8,128)(2,1)} %param.9, bf16[768,4096]{1,0:T(8,128)(2,1)} %all-gather.2.cloned.1.call-done, bf16[1,4096,512]{2,1,0:T(8,128)(2,1)} %param.8), kind=kOutput, calls=%fused_computation | convolution fusion | flops 6449135616 | bytes 20971520 | tf_op jit(solution)/shard_map/dot_general | solution.py:39
  96.5 0.0 copy-start.2
  96.5 0.0 copy-start.1
  96.5 0.0 reduce-scatter.2.cloned.1.call-update
  96.5 0.7 copy-done.2
  97.2 0.1 fusion.45
  97.4 29.9 %psum.14 = f32[256,16]{0,1:T(8,128)S(1)} all-reduce(f32[256,16]{0,1:T(8,128)S(1)} %fusion.45), channel_id=1, replica_groups=mesh['dp'=16,'expert_0'=8,'expert_1'=2] {'expert_0'}, use_global_device_ids=true, to_apply=%region_3.4 | all-reduce | flops 4096 | bytes 32768 | tf_op jit(solution)/shard_map/psum | solution.py:12
  127.3 3.3 %psum.15 = f32[256,16]{0,1:T(8,128)S(1)} all-reduce(f32[256,16]{0,1:T(8,128)S(1)} %psum.14), channel_id=1, replica_groups=mesh['dp'=16,'expert_0'=8,'expert_1'=2] {'expert_1'}, use_global_device_ids=true, to_apply=%region_4.5 | all-reduce | flops 4096 | bytes 32768 | tf_op jit(solution)/shard_map/psum | solution.py:12
  130.6 32.4 %reduce-scatter.2.cloned.1.call-done = bf16[768,256]{1,0:T(8,128)(2,1)} async-done(((bf16[768,4096]{1,0:T(8,128)(2,1)}), bf16[768,256]{1,0:T(8,128)(2,1)}) %reduce-scatter.2.cloned.1.call-update) | async-done | bytes 393232 | tf_op jit(solution)/shard_map/reduce_scatter | solution.py:40
  163.0 7.3 %all-to-all-start.1 = ((bf16[16,48,256]{2,1,0:T(8,128)(2,1)}), bf16[16,48,256]{2,1,0:T(8,128)(2,1)S(1)}, u32[]{:S(2)}, u32[]{:S(2)}) async-start(bf16[16,48,256]{2,1,0:T(8,128)(2,1)} %bitcast.47), calls=%async_computation.2 | async-start | bytes 786432 | tf_op jit(solution)/shard_map/all_to_all | solution.py:72
  170.3 0.0 copy-done.1
  170.4 8.0 %all-to-all-done.1 = bf16[16,48,256]{2,1,0:T(8,128)(2,1)S(1)} async-done(((bf16[16,48,256]{2,1,0:T(8,128)(2,1)}), bf16[16,48,256]{2,1,0:T(8,128)(2,1)S(1)}, u32[]{:S(2)}, u32[]{:S(2)}) %all-to-all-start.1) | async-done | bytes 393248 | tf_op jit(solution)/shard_map/all_to_all | solution.py:72
  178.4 1.0 convolution_convert_fusion.2
  (11 shorter events, 0.2 us)
Async XLA Ops:
  6.5 3.0 %copy-start = (bf16[256,256]{1,0:T(8,128)(2,1)S(1)}, bf16[256,256]{1,0:T(8,128)(2,1)}, u32[]{:S(2)}) copy-start(bf16[256,256]{1,0:T(8,128)(2,1)} %param.5) | copy-start | bytes 393220
  6.5 76.8 %all-gather.2.cloned.1.call-start = ((), (), s32[]{:S(2)}) async-start(), calls=%async_computation.3 | async-start | bytes 6684672 | tf_op jit(solution)/shard_map/all_gather | solution.py:34
  26.3 136.8 %reduce-scatter.2.cloned.1.call-start = ((), (), s32[]{:S(2)}) async-start(), calls=%async_computation.4 | async-start | bytes 6684672 | tf_op jit(solution)/shard_map/reduce_scatter | solution.py:40
  96.5 0.7 copy-start.2
  96.5 73.8 %copy-start.1 = (s32[256,2]{0,1:T(2,128)S(1)}, s32[256,2]{0,1:T(2,128)}, u32[]{:S(2)}) copy-start(s32[256,2]{0,1:T(2,128)} %param.6) | copy-start | bytes 6148
  163.0 15.3 %all-to-all-start.1 = ((bf16[16,48,256]{2,1,0:T(8,128)(2,1)}), bf16[16,48,256]{2,1,0:T(8,128)(2,1)S(1)}, u32[]{:S(2)}, u32[]{:S(2)}) async-start(bf16[16,48,256]{2,1,0:T(8,128)(2,1)} %bitcast.47), calls=%async_computation.2 | async-start | bytes 786432 | tf_op jit(solution)/shard_map/all_to_all | solution.py:72
Sparse Core Ops, SparseCore 0:
  26.4 56.8 all-gather.1
  96.7 66.3 reduce-scatter.1
where the time goes:
time: 187 us; the launch traced here: 186 us
  waiting for transfers between devices  97.4 us (52%)
  blocking collectives  49.3 us (26%)
  matrix products  15 us (8%)
  between operations  13.5 us (7%)
  starting transfers between devices  7.33 us (4%)
  other arithmetic  2.06 us (1%)
    all_gather x1, waiting for transfers between devices, expert_rows(): lax.all_gather(flat_rows, EXPERT, axis=1, tiled=True)  57 us
    psum x2, blocking collectives, over_axes(): value = lax.psum(value, axis)  33.2 us
    reduce_scatter x1, waiting for transfers between devices, expert_rows(): lax.psum_scatter(partial_out.astype(jnp.bfloat16), EXPERT, scatter_dimens...  32.4 us
    all_to_all x1, blocking collectives, shards(): lax.all_to_all(outgoing, 'dp', split_axis=0, concat_axis=0, tiled=True)  16.1 us
    dot_general x1, matrix products, expert_rows(): jnp.dot(hidden, weight_out, preferred_element_type=jnp.float32)  13.2 us
    all_to_all x1, waiting for transfers between devices, shards(): lax.all_to_all(processed, 'dp', split_axis=0, concat_axis=0, tiled=True)  7.96 us
    all_to_all x1, starting transfers between devices, shards(): lax.all_to_all(processed, 'dp', split_axis=0, concat_axis=0, tiled=True)  7.29 us
  transfers between devices with their start and end apart: 3, of which 3 were waited for; matrix products, arithmetic and copies ran while one was open for 0% of the time, Pallas kernels for 0%

commit v1 on v0

--- a/solution.py
+++ b/solution.py
@@ -31,7 +31,9 @@
     width_local = block_rows.shape[2]
     flat_rows = block_rows.reshape(sources * slots_here, width_local)
     pre_act = jnp.dot(
-        lax.all_gather(flat_rows, EXPERT, axis=1, tiled=True),
+        jnp.concatenate(
+            lax.all_to_all(jnp.stack([flat_rows] * lax.axis_size(EXPERT)), EXPERT, 0, 0), axis=1
+        ),
         weight_in,
         preferred_element_type=jnp.float32,
     )

time: 187 us -> 275 us (1.47)
  blocking collectives: 49.3 us -> 195 us
  waiting for transfers between devices: 97.4 us -> 39.2 us
    all_to_all x0 -> x1, blocking collectives: none -> 148 us  [expert_rows(): lax.all_to_all(jnp.stack([flat_rows] * lax.axis_size(EXPERT)), EXPERT, 0, 0)]
    all_gather x1 -> x0, waiting for transfers between devices: 57 us -> none  [expert_rows(): lax.all_gather(flat_rows, EXPERT, axis=1, tiled=True)]
  transfers between devices with their start and end apart: 3 -> 2, of which waited for: 3 -> 2; matrix products, arithmetic and copies ran while one was open for 0% -> 0% of each run, Pallas kernels for 0% -> 0%
where the time goes in v1:
time: 275 us
  blocking collectives  195 us (71%)
  waiting for transfers between devices  39.2 us (14%)
  matrix products  15.1 us (5%)
  between operations  13.5 us (5%)
  starting transfers between devices  7.5 us (3%)
    all_to_all x1, blocking collectives, expert_rows(): lax.all_to_all(jnp.stack([flat_rows] * lax.axis_size(EXPERT)), EXPERT, 0, 0)  148 us
    reduce_scatter x1, waiting for transfers between devices, expert_rows(): lax.psum_scatter(partial_out.astype(jnp.bfloat16), EXPERT, scatter_dimens...  31.2 us
    psum x2, blocking collectives, over_axes(): value = lax.psum(value, axis)  31.1 us
    all_to_all x1, blocking collectives, shards(): lax.all_to_all(outgoing, 'dp', split_axis=0, concat_axis=0, tiled=True)  16 us
    dot_general x1, matrix products, expert_rows(): jnp.dot(hidden, weight_out, preferred_element_type=jnp.float32)  13.3 us
    all_to_all x1, waiting for transfers between devices, shards(): lax.all_to_all(processed, 'dp', split_axis=0, concat_axis=0, tiled=True)  7.96 us
    all_to_all x1, starting transfers between devices, shards(): lax.all_to_all(processed, 'dp', split_axis=0, concat_axis=0, tiled=True)  7.5 us
  transfers between devices with their start and end apart: 2, of which 2 were waited for; matrix products, arithmetic and copies ran while one was open for 0% of the time, Pallas kernels for 0%

profile of v1, /device:TPU:2, one launch (start us, length us, event | category | flops | bytes accessed | tf_op | source)
XLA Modules:
  0.0 274.8 jit_solution(15729630038480206925)
XLA Ops:
  6.5 0.0 copy-start
  6.5 0.0 reduce-scatter.2.cloned.1.call-start
  6.5 0.8 fusion.40
  7.3 1.2 reduce-window.6
  8.5 0.2 slice_reduce_fusion
  8.7 0.1 fusion.31
  8.9 0.7 add_add_fusion
  9.6 0.0 copy-done
  9.6 0.6 convolution_convert_fusion.1
  10.2 16.0 %all_to_all.15 = bf16[16,48,256]{2,1,0:T(8,128)(2,1)S(1)} all-to-all(bf16[16,48,256]{2,1,0:T(8,128)(2,1)S(1)} %bitcast.53), channel_id=1, replica_groups=mesh['dp'=16,'expert_0'=8,'expert_1'=2] {'dp'}, dimensions={0} | all-to-all | bytes 786432 | tf_op jit(solution)/shard_map/all_to_all | solution.py:72
  26.2 0.2 copy.13
  26.3 0.6 stack.15
  26.9 148.0 %all_to_all.16 = bf16[16,768,256]{1,2,0:T(8,128)(2,1)} all-to-all(bf16[16,768,256]{1,2,0:T(8,128)(2,1)S(1)} %stack.15), channel_id=1, replica_groups=mesh['dp'=16,'expert_0'=8,'expert_1'=2] {'expert_0','expert_1'}, dimensions={0} | all-to-all | bytes 12582912 | tf_op jit(solution)/shard_map/all_to_all | solution.py:35
  175.0 13.3 %convolution_convert_fusion = bf16[768,4096]{1,0:T(8,128)(2,1)} fusion(bf16[1,512,4096]{2,1,0:T(8,128)(2,1)} %param.9, bf16[768,4096]{0,1:T(8,128)(2,1)} %bitcast.49, bf16[1,4096,512]{2,1,0:T(8,128)(2,1)} %param.8), kind=kOutput, calls=%fused_computation | convolution fusion | flops 6449135616 | bytes 20971520 | tf_op jit(solution)/shard_map/dot_general | solution.py:41
  188.3 0.0 copy-start.2
  188.3 0.0 copy-start.1
  188.3 0.0 reduce-scatter.2.cloned.1.call-update
  188.3 0.7 copy-done.2
  189.0 0.1 fusion.41
  189.1 27.7 %psum.14 = f32[256,16]{0,1:T(8,128)S(1)} all-reduce(f32[256,16]{0,1:T(8,128)S(1)} %fusion.41), channel_id=1, replica_groups=mesh['dp'=16,'expert_0'=8,'expert_1'=2] {'expert_0'}, use_global_device_ids=true, to_apply=%region_3.4 | all-reduce | flops 4096 | bytes 32768 | tf_op jit(solution)/shard_map/psum | solution.py:12
  216.9 3.3 %psum.15 = f32[256,16]{0,1:T(8,128)S(1)} all-reduce(f32[256,16]{0,1:T(8,128)S(1)} %psum.14), channel_id=1, replica_groups=mesh['dp'=16,'expert_0'=8,'expert_1'=2] {'expert_1'}, use_global_device_ids=true, to_apply=%region_4.5 | all-reduce | flops 4096 | bytes 32768 | tf_op jit(solution)/shard_map/psum | solution.py:12
  220.2 31.2 %reduce-scatter.2.cloned.1.call-done = bf16[768,256]{1,0:T(8,128)(2,1)} async-done(((bf16[768,4096]{1,0:T(8,128)(2,1)}), bf16[768,256]{1,0:T(8,128)(2,1)}) %reduce-scatter.2.cloned.1.call-update) | async-done | bytes 393232 | tf_op jit(solution)/shard_map/reduce_scatter | solution.py:42
  251.4 7.5 %all-to-all-start.2 = ((bf16[16,48,256]{2,1,0:T(8,128)(2,1)}), bf16[16,48,256]{2,1,0:T(8,128)(2,1)S(1)}, u32[]{:S(2)}, u32[]{:S(2)}) async-start(bf16[16,48,256]{2,1,0:T(8,128)(2,1)} %bitcast.51), calls=%async_computation.3 | async-start | bytes 786432 | tf_op jit(solution)/shard_map/all_to_all | solution.py:74
  258.9 0.0 copy-done.1
  259.0 8.0 %all-to-all-done.2 = bf16[16,48,256]{2,1,0:T(8,128)(2,1)S(1)} async-done(((bf16[16,48,256]{2,1,0:T(8,128)(2,1)}), bf16[16,48,256]{2,1,0:T(8,128)(2,1)S(1)}, u32[]{:S(2)}, u32[]{:S(2)}) %all-to-all-start.2) | async-done | bytes 393248 | tf_op jit(solution)/shard_map/all_to_all | solution.py:74
  267.0 1.0 convolution_convert_fusion.2
  (11 shorter events, 0.2 us)
Async XLA Ops:
  6.5 3.0 %copy-start = (bf16[256,256]{1,0:T(8,128)(2,1)S(1)}, bf16[256,256]{1,0:T(8,128)(2,1)}, u32[]{:S(2)}) copy-start(bf16[256,256]{1,0:T(8,128)(2,1)} %param.5) | copy-start | bytes 393220
  6.5 244.9 %reduce-scatter.2.cloned.1.call-start = ((), (), s32[]{:S(2)}) async-start(), calls=%async_computation.4 | async-start | bytes 6684672 | tf_op jit(solution)/shard_map/reduce_scatter | solution.py:42
  188.3 0.7 copy-start.2
  188.3 70.6 %copy-start.1 = (s32[256,2]{0,1:T(2,128)S(1)}, s32[256,2]{0,1:T(2,128)}, u32[]{:S(2)}) copy-start(s32[256,2]{0,1:T(2,128)} %param.6) | copy-start | bytes 6148
  251.4 15.5 %all-to-all-start.2 = ((bf16[16,48,256]{2,1,0:T(8,128)(2,1)}), bf16[16,48,256]{2,1,0:T(8,128)(2,1)S(1)}, u32[]{:S(2)}, u32[]{:S(2)}) async-start(bf16[16,48,256]{2,1,0:T(8,128)(2,1)} %bitcast.51), calls=%async_computation.3 | async-start | bytes 786432 | tf_op jit(solution)/shard_map/all_to_all | solution.py:74
Sparse Core Ops, SparseCore 0:
  188.4 62.9 reduce-scatter.1
